TPU v7x, 32 devices: a whole 2x2x4 slice. The times are simulated.
32 devices in a mesh: wide: 8 (over y, x, core), narrow: 4 (over z).
Axes of the slice: x: 2, y: 2, z: 4, core: 2. Of those that a mesh axis runs over, the one named last changes fastest.
Arguments:
- momentum: float32 [9216, 9216], P('wide', 'narrow'), may hold values from -3 to 3
- gradient: bfloat16 [9216, 9216], P('wide', 'narrow'), may hold values from -48 to 48
- right_factor: float32 [512, 9216], P('wide', 'narrow'), may hold values from -6 to 6
Outputs:
- new_momentum: float32 [9216, 9216], P('wide', 'narrow')
- new_right: float32 [512, 9216], P('wide', 'narrow')
- update: bfloat16 [9216, 9216], P('wide', 'narrow')
All inputs are finite; a program needn't handle non-finite values.
Results may differ from a plain program's by a relative error of at most 0.001.
Values sent between devices are 32-bit elements; how exact they have to be, the bound alone decides.
No kernel may reach another device: no remote copies, remote signals or barrier semaphores. Data moves between devices by JAX's collectives and lax.ppermute only.
A program may use at most 128 MiB of HBM per device.

v0:
```python
import jax
import jax.numpy as jnp
from jax import lax
from jax.sharding import PartitionSpec as P

N_COLS = 9216
EPS = 1e-06
MU = 0.95


def orthonormal(projected, gram_matrix):
    factor_lower = jnp.linalg.cholesky(gram_matrix)
    return jax.scipy.linalg.solve_triangular(factor_lower, projected.T, lower=True).T


def matmul(left, right):
    return jnp.dot(left, right, preferred_element_type=jnp.float32, precision=lax.Precision.HIGHEST)


def per_device(momentum, gradient, right_factor):
    blended = momentum + gradient.astype(jnp.float32)
    partial_left = matmul(blended, lax.all_gather(right_factor, "wide", axis=0, tiled=True).T)
    projected = lax.psum(partial_left, "narrow")
    gram_matrix = lax.psum(matmul(projected.T, projected), "wide")
    left_basis = orthonormal(projected, gram_matrix)
    columns = left_basis
    right_block = lax.psum_scatter(
        matmul(columns.T, blended), "wide", scatter_dimension=0, tiled=True
    )
    squares = lax.psum(jnp.sum(right_block * right_block, axis=1), "narrow")
    root_mean = jnp.sqrt(squares / N_COLS + EPS)
    new_right = right_block / root_mean[:, None]
    pieces = (
        lax.all_gather(right_block, "wide", axis=0, tiled=True),
        lax.all_gather(root_mean, "wide", axis=0, tiled=True),
    )
    columns = left_basis
    normed = pieces[0] / pieces[1][:, None]
    feedback = matmul(columns, pieces[0])
    direction = matmul(columns, normed)
    new_momentum = blended - (1.0 - MU) * feedback
    return (new_momentum, new_right, direction.astype(jnp.bfloat16))


def solution(mesh):
    return jax.shard_map(
        per_device,
        mesh=mesh,
        in_specs=(P("wide", "narrow"), P("wide", "narrow"), P("wide", "narrow")),
        out_specs=(P("wide", "narrow"), P("wide", "narrow"), P("wide", "narrow")),
        check_vma=False,
    )
```

profile of v0, /device:TPU:0, one launch (start us, length us, event | category | flops | bytes accessed | tf_op | source)
XLA Modules:
  0.0 566.0 jit_solution(15770033689719844626)
XLA Ops:
  7.2 0.7 all-gather.3.cloned.1.call-update
  7.9 43.5 %all-gather.3.cloned.1.call-done = f32[512,2304]{1,0:T(8,128)} async-done(((f32[64,2304]{1,0:T(8,128)}), f32[512,2304]{1,0:T(8,128)}) %all-gather.3.cloned.1.call-update) | async-done | bytes 4718608 | tf_op jit(solution)/shard_map/all_gather | solution.py:22
  51.4 22.9 %fusion.3 = f32[1152,512]{1,0:T(8,128)} fusion(f32[512,2304]{1,0:T(8,128)} %all-gather.3.cloned.1.call-done, f32[1152,2304]{1,0:T(8,128)} %param.3, bf16[1152,2304]{1,0:T(8,128)(2,1)} %param.4), kind=kOutput, calls=%fused_computation.8 | convolution fusion | flops 16312762368 | bytes 23003136 | tf_op jit(solution)/shard_map/dot_general | solution.py:17
  74.3 0.0 all-reduce.7.cloned.1.call-start
  74.4 94.7 %all-reduce.5.cloned.1.call-done = f32[1152,512]{1,0:T(8,128)} async-done(((f32[1152,512]{1,0:T(8,128)}), f32[1152,512]{1,0:T(8,128)}) %all-reduce.5.cloned.1.call-update) | async-done | bytes 2359312 | tf_op jit(solution)/shard_map/psum | solution.py:23
  169.1 7.7 %fusion.40 = f32[512,512]{0,1:T(8,128)} fusion(f32[1152,512]{1,0:T(8,128)} %all-reduce.5.cloned.1.call-done), kind=kOutput, calls=%fused_computation.82 | convolution fusion | flops 3623878656 | bytes 3407872 | tf_op jit(solution)/shard_map/dot_general | solution.py:17
  176.8 0.3 reduce-scatter.2.cloned.1.call-start
  177.1 55.6 %all-reduce.7.cloned.1.call-done = f32[512,512]{0,1:T(8,128)} async-done(((f32[512,512]{0,1:T(8,128)}), f32[512,512]{0,1:T(8,128)}) %all-reduce.7.cloned.1.call-update) | async-done | bytes 1048592 | tf_op jit(solution)/shard_map/psum | solution.py:24
  232.7 1.6 copy.7
  234.3 0.2 fusion.13
  234.6 1.0 copy-done.5
  235.6 11.7 %cholesky.104 = f32[128,128]{1,0:T(8,128)S(1)} custom-call(f32[128,128]{1,0:T(8,128)S(1)} %cholesky.266), custom_call_target="Cholesky" | custom-call | tf_op jit(solution)/shard_map/jit(cholesky)/cholesky | solution.py:12
  247.3 9.8 %custom-call.31 = f32[1,128,128]{1,2,0:T(8,128)S(1)} custom-call(f32[1,128,128]{2,1,0:T(8,128)S(1)} %get-tuple-element.30), custom_call_target="InvertDiagBlocksLowerTriangular" | custom-call | tf_op jit(solution)/shard_map/jit(cholesky)/cholesky | solution.py:12
  257.1 0.1 cholesky.224
  257.2 1.2 constant_dynamic-update-slice_fusion.3
  258.5 1.3 convolution_subtract_fusion.3
  259.8 11.7 %cholesky.217 = f32[128,128]{1,0:T(8,128)S(1)} custom-call(f32[128,128]{1,0:T(8,128)S(1)} %cholesky.270), custom_call_target="Cholesky" | custom-call | tf_op jit(solution)/shard_map/jit(cholesky)/cholesky | solution.py:12
  271.5 10.2 %custom-call.32 = f32[1,128,128]{1,2,0:T(8,128)S(1)} custom-call(f32[1,128,128]{2,1,0:T(8,128)S(1)} %get-tuple-element.27), custom_call_target="InvertDiagBlocksLowerTriangular" | custom-call | tf_op jit(solution)/shard_map/jit(cholesky)/cholesky | solution.py:12
  281.7 0.3 convolution_dynamic-update-slice_fusion
  282.0 1.4 convolution_subtract_fusion.4
  283.4 0.6 cholesky.275
  284.1 13.2 %cholesky.238 = f32[128,128]{1,0:T(8,128)} custom-call(f32[128,128]{1,0:T(8,128)} %cholesky.275), custom_call_target="Cholesky" | custom-call | tf_op jit(solution)/shard_map/jit(cholesky)/cholesky | solution.py:12
  297.2 1.5 select_reduce_fusion.1
  298.7 0.7 compare_reduce_fusion.1
  299.4 11.3 %custom-call.33 = f32[1,128,128]{1,2,0:T(8,128)} custom-call(f32[1,128,128]{2,1,0:T(8,128)} %get-tuple-element.24), custom_call_target="InvertDiagBlocksLowerTriangular" | custom-call | tf_op jit(solution)/shard_map/jit(cholesky)/cholesky | solution.py:12
  310.7 1.0 convolution_dynamic-update-slice_fusion.1
  311.8 1.2 convolution_subtract_fusion.5
  313.0 11.7 %cholesky.255 = f32[128,128]{1,0:T(8,128)S(1)} custom-call(f32[128,128]{1,0:T(8,128)S(1)} %convolution_subtract_fusion.5), custom_call_target="Cholesky" | custom-call | tf_op jit(solution)/shard_map/jit(cholesky)/cholesky | solution.py:12
  324.7 0.6 compare_reduce_fusion
  325.4 0.6 compare_reduce_fusion.2
  328.5 1.3 select_select_fusion
  329.8 13.7 %while.1 = (s32[]{:T(128)}, f32[512,512]{1,0:T(8,128)}, s32[4,2]{0,1:T(2,128)S(1)}, f32[4,128,128]{2,1,0:T(8,128)}, s32[]{:T(128)}) while((s32[]{:T(128)}, f32[512,512]{1,0:T(8,128)}, s32[4,2]{0,1:T(2,128)S(1)}, f32[4,128,128]{2,1,0:T(8,128)}, s32[]{:T(128)}) %tuple.32), condition=%wide.while_cond, body=%wide.while_body.sunk | while | flops 2 | bytes 132205 | solution.py:13
  329.8 0.1 constant_dynamic-slice_fusion.2
  329.9 0.5 fusion.51
  330.4 2.8 bitcast_dynamic-update-slice_fusion.2
  333.2 0.1 constant_dynamic-slice_fusion.2
  333.3 0.5 fusion.51
  333.8 2.8 bitcast_dynamic-update-slice_fusion.2
  336.7 0.1 constant_dynamic-slice_fusion.2
  336.7 0.5 fusion.51
  337.3 2.8 bitcast_dynamic-update-slice_fusion.2
  340.1 0.1 constant_dynamic-slice_fusion.2
  340.2 0.5 fusion.51
  340.7 2.8 bitcast_dynamic-update-slice_fusion.2
  343.5 40.1 %custom-call.34 = f32[4,128,128]{1,2,0:T(8,128)S(1)} custom-call(f32[4,128,128]{2,1,0:T(8,128)} %get-tuple-element.10), custom_call_target="InvertDiagBlocksLowerTriangular" | custom-call | tf_op jit(solution)/shard_map/jit(_solve_triangular)/triangular_solve | solution.py:13
  383.6 0.7 fusion.14
  384.4 2.4 convolution_subtract_fusion.2
  386.8 1.6 fusion.27
  388.4 3.0 convolution_subtract_fusion.1
  391.5 0.7 fusion.25
  392.2 4.2 convolution_subtract_fusion
  396.5 0.7 fusion.24
  397.3 23.1 %fusion.2 = f32[512,2304]{1,0:T(8,128)} fusion(f32[1152,2304]{1,0:T(8,128)} %param.3, bf16[1152,2304]{1,0:T(8,128)(2,1)S(1)} %bitcast.55, f32[128,1152]{1,0:T(8,128)S(1)} %fusion.24, f32[128,1152]{1,0:T(8,128)S(1)} %fusion.25, f32[128,1152]{1,0:T(8,128)S(1)} %fusion.27, f32[128,1152]{1,0:T(8,128)S(1)} %fusion.14), kind=kOutput, calls=%fused_computation.7 | convolution fusion | flops 16314531840 | bytes 23003136 | tf_op jit(solution)/shard_map/dot_general | solution.py:17
  420.4 0.0 all-gather.5.cloned.1.call-start
  420.4 53.1 %reduce-scatter.2.cloned.1.call-done = f32[64,2304]{1,0:T(8,128)} async-done(((f32[512,2304]{1,0:T(8,128)}), f32[64,2304]{1,0:T(8,128)}) %reduce-scatter.2.cloned.1.call-update) | async-done | bytes 589840 | tf_op jit(solution)/shard_map/reduce_scatter | solution.py:27
  473.6 0.6 dynamic-slice.3
  474.8 1.2 multiply_reduce_fusion
  476.0 11.7 %psum.23 = f32[64]{0:T(128)S(1)} all-reduce(f32[64]{0:T(128)S(1)} %multiply_reduce_fusion), channel_id=1, replica_groups=mesh['wide'=8,'narrow'=4] {'narrow'}, use_global_device_ids=true, to_apply=%region_12.13 | all-reduce | flops 64 | bytes 512 | tf_op jit(solution)/shard_map/psum | solution.py:30
  487.7 0.1 fusion.38
  487.8 12.1 %all-reduce.1 = f32[512]{0:T(512)S(1)} all-reduce(f32[512]{0:T(512)S(1)} %get-tuple-element.31), channel_id=1, replica_groups=mesh['wide'=8,'narrow'=4] {'wide'}, use_global_device_ids=true, to_apply=%add.1 | all-reduce | flops 512 | bytes 4096
  499.9 2.0 broadcast_divide_fusion
  501.9 12.3 %all-gather.5.cloned.1.call-done = f32[512,2304]{1,0:T(8,128)} async-done(((f32[64,2304]{1,0:T(8,128)}), f32[512,2304]{1,0:T(8,128)}) %all-gather.5.cloned.1.call-update) | async-done | bytes 4718608 | tf_op jit(solution)/shard_map/all_gather | solution.py:34
  514.2 24.1 %fusion = f32[1152,2304]{1,0:T(8,128)} fusion(f32[512,2304]{1,0:T(8,128)} %all-gather.5.cloned.1.call-done, f32[1152,2304]{1,0:T(8,128)} %param.3, bf16[1152,2304]{1,0:T(8,128)(2,1)} %param.4, f32[128,1152]{1,0:T(8,128)S(1)} %fusion.24, f32[128,1152]{1,0:T(8,128)S(1)} %copy-done.2, f32[128,1152]{1,0:T(8,128)S(1)} %fusion.27, f32[128,1152]{1,0:T(8,128)S(1)} %fusion.14), kind=kOutput, calls=%fused_computation.3 | convolution fusion | flops 16319840256 | bytes 33619968 | tf_op jit(solution)/shard_map/dot_general | solution.py:17
  538.3 20.7 %convolution_convert_fusion = bf16[1152,2304]{1,0:T(8,128)(2,1)} fusion(f32[512,2304]{1,0:T(8,128)S(1)} %copy-done.3, f32[512]{0:T(512)S(1)} %all-reduce.1, f32[128,1152]{1,0:T(8,128)S(1)} %fusion.24, f32[128,1152]{1,0:T(8,128)S(1)} %copy-done.2, f32[128,1152]{1,0:T(8,128)S(1)} %fusion.27, f32[128,1152]{1,0:T(8,128)S(1)} %fusion.14), kind=kOutput, calls=%fused_computation.4 | convolution fusion | flops 16313057280 | bytes 12388352 | tf_op jit(solution)/shard_map/dot_general | solution.py:17
  (37 shorter events, 0.3 us)
Async XLA Ops:
  7.2 44.2 %all-gather.3.cloned.1.call-start = ((), (), s32[]{:S(2)}) async-start(), calls=%async_computation.1 | async-start | bytes 5308416 | tf_op jit(solution)/shard_map/all_gather | solution.py:22
  7.9 161.2 %all-reduce.5.cloned.1.call-start = ((), (), s32[]{:S(2)}) async-start(), calls=%async_computation.2 | async-start | bytes 4718592 | tf_op jit(solution)/shard_map/psum | solution.py:23
  74.3 158.4 %all-reduce.7.cloned.1.call-start = ((), (), s32[]{:S(2)}) async-start(), calls=%async_computation.3 | async-start | bytes 2097152 | tf_op jit(solution)/shard_map/psum | solution.py:24
  176.8 296.7 %reduce-scatter.2.cloned.1.call-start = ((), (), s32[]{:S(2)}) async-start(), calls=%async_computation.4 | async-start | bytes 5308416 | tf_op jit(solution)/shard_map/reduce_scatter | solution.py:27
  232.7 1.7 copy-start.4
  234.6 1.0 copy-start.5
  282.0 101.6 %copy-start = (f32[1152,512]{1,0:T(8,128)S(1)}, f32[1152,512]{1,0:T(8,128)}, u32[]{:S(2)}) copy-start(f32[1152,512]{1,0:T(8,128)} %all-reduce.5.cloned.1.call-done) | copy-start | bytes 7077892
  383.6 0.8 copy-start.6
  383.6 13.6 %slice-start = ((s8[5308416]{0:T(1024)(128)(4,1)}), s8[4194304]{0:T(1024)(128)(4,1)S(1)}, s32[]{:S(2)}) async-start(s8[5308416]{0:T(1024)(128)(4,1)} %bitcast.54), calls=%async_computation.6 | async-start | bytes 8388608
  386.8 4.7 copy-start.7
  388.4 8.8 %slice-start.1 = ((s8[5308416]{0:T(1024)(128)(4,1)}), s8[1114112]{0:T(1024)(128)(4,1)S(1)}, s32[]{:S(2)}) async-start(s8[5308416]{0:T(1024)(128)(4,1)} %bitcast.54), calls=%async_computation.7 | async-start | bytes 2228224
  392.2 5.0 copy-start.1
  420.3 53.2 %copy-start.8 = (u32[32]{0:T(128)S(1)}, u32[32]{0:T(128)}, u32[]{:S(2)}) copy-start(u32[32]{0:T(128)} %constant.172) | copy-start | bytes 388
  420.4 93.8 %copy-start.2 = (f32[128,1152]{1,0:T(8,128)S(1)}, f32[128,1152]{1,0:T(8,128)}, u32[]{:S(2)}) copy-start(f32[128,1152]{1,0:T(8,128)} %copy-done.1) | copy-start | bytes 1769476
  420.4 93.8 %all-gather.5.cloned.1.call-start = ((), (), s32[]{:S(2)}) async-start(), calls=%async_computation.5 | async-start | bytes 5308416 | tf_op jit(solution)/shard_map/all_gather | solution.py:34
  514.2 24.1 %copy-start.3 = (f32[512,2304]{1,0:T(8,128)S(1)}, f32[512,2304]{1,0:T(8,128)}, u32[]{:S(2)}) copy-start(f32[512,2304]{1,0:T(8,128)} %all-gather.5.cloned.1.call-done) | copy-start | bytes 14155780
Sparse Core Ops, SparseCore 0:
  9.9 41.4 all-gather.2
  74.4 94.6 all-reduce.4
  176.9 55.7 all-reduce.6
  420.5 53.0 reduce-scatter.1
  475.3 38.9 all-gather.4
where the time goes:
time: 574 us; the launch traced here: 566 us
  waiting for transfers between devices  260 us (45%)
  other arithmetic  128 us (22%)
  matrix products  118 us (21%)
  blocking collectives  23.8 us (4%)
  between operations  17.8 us (3%)
  local copies, waits for them, and re-layouts  17.7 us (3%)
    dot_general x5, matrix products, matmul(): jnp.dot(left, right, preferred_element_type=jnp.float32, precision=lax.Pr...  98.4 us
    psum x1, waiting for transfers between devices, per_device(): projected = lax.psum(partial_left, 'narrow')  94.7 us
    another operation x14, other arithmetic, orthonormal(): factor_lower = jnp.linalg.cholesky(gram_matrix)  83.1 us
    psum x1, waiting for transfers between devices, per_device(): gram_matrix = lax.psum(matmul(projected.T, projected), 'wide')  55.6 us
    reduce_scatter x1, waiting for transfers between devices, per_device(): lax.psum_scatter(matmul(columns.T, blended), 'wide', scatter_dimension=0,...  53.1 us
    all_gather x1, waiting for transfers between devices, per_device(): lax.all_gather(right_factor, 'wide', axis=0, tiled=True)  43.5 us
    another operation x3, other arithmetic, orthonormal(): jax.scipy.linalg.solve_triangular(factor_lower, projected.T, lower=True)  41.4 us
    another operation x12, local copies, waits for them, and re-layouts  13.7 us
  transfers between devices with their start and end apart: 5, of which 5 were waited for; matrix products, arithmetic and copies ran while one was open for 1% of the time, Pallas kernels for 0%

commit v1 on v0

--- a/solution.py
+++ b/solution.py
@@ -18,9 +18,14 @@
 
 
 def per_device(momentum, gradient, right_factor):
+
+    def _unite_space(original, axis_tag):
+        latest = jnp.sum(lax.all_gather(original, axis_tag), axis=0)
+        return latest
+
     blended = momentum + gradient.astype(jnp.float32)
     partial_left = matmul(blended, lax.all_gather(right_factor, "wide", axis=0, tiled=True).T)
-    projected = lax.psum(partial_left, "narrow")
+    projected = _unite_space(partial_left, "narrow")
     gram_matrix = lax.psum(matmul(projected.T, projected), "wide")
     left_basis = orthonormal(projected, gram_matrix)
     columns = left_basis

time: 574 us -> 654 us (1.14)
  waiting for transfers between devices: 260 us -> 331 us
    all_gather x0 -> x1, waiting for transfers between devices: none -> 167 us  [_unite_space(): latest = jnp.sum(lax.all_gather(original, axis_tag), axis=0)]
    psum x1 -> x0, waiting for transfers between devices: 94.7 us -> none  [per_device(): projected = lax.psum(partial_left, 'narrow')]
where the time goes in v1:
time: 654 us; the launch traced here: 645 us
  waiting for transfers between devices  331 us (51%)
  other arithmetic  134 us (20%)
  matrix products  117 us (18%)
  blocking collectives  23.8 us (4%)
  local copies, waits for them, and re-layouts  20.1 us (3%)
  between operations  17.8 us (3%)
    all_gather x1, waiting for transfers between devices, _unite_space(): latest = jnp.sum(lax.all_gather(original, axis_tag), axis=0)  167 us
    dot_general x5, matrix products, matmul(): jnp.dot(left, right, preferred_element_type=jnp.float32, precision=lax.Pr...  96 us
    another operation x14, other arithmetic, orthonormal(): factor_lower = jnp.linalg.cholesky(gram_matrix)  83.2 us
    psum x1, waiting for transfers between devices, per_device(): gram_matrix = lax.psum(matmul(projected.T, projected), 'wide')  54.8 us
    reduce_scatter x1, waiting for transfers between devices, per_device(): lax.psum_scatter(matmul(columns.T, blended), 'wide', scatter_dimension=0,...  53.1 us
    all_gather x1, waiting for transfers between devices, per_device(): lax.all_gather(right_factor, 'wide', axis=0, tiled=True)  43.5 us
    another operation x3, other arithmetic, orthonormal(): jax.scipy.linalg.solve_triangular(factor_lower, projected.T, lower=True)  41.4 us
    another operation x12, local copies, waits for them, and re-layouts  14.5 us
  transfers between devices with their start and end apart: 5, of which 5 were waited for; matrix products, arithmetic and copies ran while one was open for 1% of the time, Pallas kernels for 0%

profile of v1, /device:TPU:0, one launch (start us, length us, event | category | flops | bytes accessed | tf_op | source)
XLA Modules:
  0.0 644.6 jit_solution(4743406619204210991)
XLA Ops:
  7.2 0.7 all-gather.5.cloned.1.call-update
  7.9 43.5 %all-gather.5.cloned.1.call-done = f32[512,2304]{1,0:T(8,128)} async-done(((f32[64,2304]{1,0:T(8,128)}), f32[512,2304]{1,0:T(8,128)}) %all-gather.5.cloned.1.call-update) | async-done | bytes 4718608 | tf_op jit(solution)/shard_map/all_gather | solution.py:27
  51.4 22.9 %fusion.3 = f32[1152,512]{1,0:T(8,128)} fusion(f32[512,2304]{1,0:T(8,128)} %all-gather.5.cloned.1.call-done, f32[1152,2304]{1,0:T(8,128)} %param.3, bf16[1152,2304]{1,0:T(8,128)(2,1)} %param.4), kind=kOutput, calls=%fused_computation.8 | convolution fusion | flops 16312762368 | bytes 23003136 | tf_op jit(solution)/shard_map/dot_general | solution.py:17
  74.4 166.9 %all-gather.9.cloned.1.call-done = f32[4608,512]{1,0:T(8,128)} async-done(((f32[1152,512]{1,0:T(8,128)}), f32[4608,512]{1,0:T(8,128)}) %all-gather.9.cloned.1.call-update) | async-done | bytes 9437200 | tf_op jit(solution)/shard_map/all_gather | solution.py:23
  241.2 5.1 reduce_sum.18
  246.3 5.3 fusion.40
  251.7 0.3 reduce-scatter.2.cloned.1.call-start
  252.0 54.8 %all-reduce.4.cloned.1.call-done = f32[512,512]{0,1:T(8,128)} async-done(((f32[512,512]{0,1:T(8,128)}), f32[512,512]{0,1:T(8,128)}) %all-reduce.4.cloned.1.call-update) | async-done | bytes 1048592 | tf_op jit(solution)/shard_map/psum | solution.py:29
  306.7 2.6 copy.7
  309.3 1.4 fusion.13
  310.8 1.0 copy-done.4
  311.8 11.7 %cholesky.104 = f32[128,128]{1,0:T(8,128)S(1)} custom-call(f32[128,128]{1,0:T(8,128)S(1)} %cholesky.266), custom_call_target="Cholesky" | custom-call | tf_op jit(solution)/shard_map/jit(cholesky)/cholesky | solution.py:12
  323.5 0.1 cholesky.224
  323.7 9.8 %custom-call.31 = f32[1,128,128]{1,2,0:T(8,128)S(1)} custom-call(f32[1,128,128]{2,1,0:T(8,128)S(1)} %get-tuple-element.30), custom_call_target="InvertDiagBlocksLowerTriangular" | custom-call | tf_op jit(solution)/shard_map/jit(cholesky)/cholesky | solution.py:12
  333.5 1.2 constant_dynamic-update-slice_fusion.3
  334.7 1.3 convolution_subtract_fusion.3
  336.0 0.7 copy-done.5
  336.7 11.7 %cholesky.217 = f32[128,128]{1,0:T(8,128)S(1)} custom-call(f32[128,128]{1,0:T(8,128)S(1)} %cholesky.270), custom_call_target="Cholesky" | custom-call | tf_op jit(solution)/shard_map/jit(cholesky)/cholesky | solution.py:12
  348.4 10.2 %custom-call.32 = f32[1,128,128]{1,2,0:T(8,128)S(1)} custom-call(f32[1,128,128]{2,1,0:T(8,128)S(1)} %get-tuple-element.27), custom_call_target="InvertDiagBlocksLowerTriangular" | custom-call | tf_op jit(solution)/shard_map/jit(cholesky)/cholesky | solution.py:12
  358.6 1.2 convolution_dynamic-update-slice_fusion
  359.8 1.3 convolution_subtract_fusion.4
  361.1 0.6 cholesky.275
  361.7 13.2 %cholesky.238 = f32[128,128]{1,0:T(8,128)} custom-call(f32[128,128]{1,0:T(8,128)} %cholesky.275), custom_call_target="Cholesky" | custom-call | tf_op jit(solution)/shard_map/jit(cholesky)/cholesky | solution.py:12
  374.9 1.5 select_reduce_fusion.1
  376.4 0.7 compare_reduce_fusion.1
  377.0 11.3 %custom-call.33 = f32[1,128,128]{1,2,0:T(8,128)} custom-call(f32[1,128,128]{2,1,0:T(8,128)} %get-tuple-element.24), custom_call_target="InvertDiagBlocksLowerTriangular" | custom-call | tf_op jit(solution)/shard_map/jit(cholesky)/cholesky | solution.py:12
  388.3 1.0 convolution_dynamic-update-slice_fusion.1
  389.4 1.2 convolution_subtract_fusion.5
  390.6 11.7 %cholesky.255 = f32[128,128]{1,0:T(8,128)S(1)} custom-call(f32[128,128]{1,0:T(8,128)S(1)} %convolution_subtract_fusion.5), custom_call_target="Cholesky" | custom-call | tf_op jit(solution)/shard_map/jit(cholesky)/cholesky | solution.py:12
  402.3 0.7 compare_reduce_fusion
  403.1 0.6 compare_reduce_fusion.2
  406.3 1.3 select_select_fusion
  407.6 14.5 %while.1 = (s32[]{:T(128)}, f32[512,512]{1,0:T(8,128)}, s32[4,2]{0,1:T(2,128)S(1)}, f32[4,128,128]{2,1,0:T(8,128)}, s32[]{:T(128)}) while((s32[]{:T(128)}, f32[512,512]{1,0:T(8,128)}, s32[4,2]{0,1:T(2,128)S(1)}, f32[4,128,128]{2,1,0:T(8,128)}, s32[]{:T(128)}) %tuple.32), condition=%wide.while_cond, body=%wide.while_body.sunk | while | flops 2 | bytes 132205 | solution.py:13
  407.6 0.1 constant_dynamic-slice_fusion.2
  407.6 0.6 fusion.51
  408.2 3.0 bitcast_dynamic-update-slice_fusion.2
  411.2 0.1 constant_dynamic-slice_fusion.2
  411.3 0.6 fusion.51
  411.9 3.0 bitcast_dynamic-update-slice_fusion.2
  414.9 0.1 constant_dynamic-slice_fusion.2
  414.9 0.6 fusion.51
  415.5 3.0 bitcast_dynamic-update-slice_fusion.2
  418.5 0.1 constant_dynamic-slice_fusion.2
  418.6 0.6 fusion.51
  419.2 2.9 bitcast_dynamic-update-slice_fusion.2
  422.1 40.1 %custom-call.34 = f32[4,128,128]{1,2,0:T(8,128)S(1)} custom-call(f32[4,128,128]{2,1,0:T(8,128)} %get-tuple-element.10), custom_call_target="InvertDiagBlocksLowerTriangular" | custom-call | tf_op jit(solution)/shard_map/jit(_solve_triangular)/triangular_solve | solution.py:13
  462.2 0.7 fusion.14
  463.0 2.4 convolution_subtract_fusion.2
  465.4 1.6 fusion.27
  467.0 3.0 convolution_subtract_fusion.1
  470.1 0.7 fusion.25
  470.8 4.2 convolution_subtract_fusion
  475.1 0.7 fusion.24
  475.9 23.1 %fusion.2 = f32[512,2304]{1,0:T(8,128)} fusion(f32[1152,2304]{1,0:T(8,128)} %param.3, bf16[1152,2304]{1,0:T(8,128)(2,1)S(1)} %bitcast.60, f32[128,1152]{1,0:T(8,128)S(1)} %fusion.24, f32[128,1152]{1,0:T(8,128)S(1)} %fusion.25, f32[128,1152]{1,0:T(8,128)S(1)} %fusion.27, f32[128,1152]{1,0:T(8,128)S(1)} %fusion.14), kind=kOutput, calls=%fused_computation.7 | convolution fusion | flops 16314531840 | bytes 23003136 | tf_op jit(solution)/shard_map/dot_general | solution.py:17
  499.0 53.1 %reduce-scatter.2.cloned.1.call-done = f32[64,2304]{1,0:T(8,128)} async-done(((f32[512,2304]{1,0:T(8,128)}), f32[64,2304]{1,0:T(8,128)}) %reduce-scatter.2.cloned.1.call-update) | async-done | bytes 589840 | tf_op jit(solution)/shard_map/reduce_scatter | solution.py:32
  552.2 0.6 dynamic-slice.3
  553.4 1.2 multiply_reduce_fusion
  554.6 11.7 %psum.15 = f32[64]{0:T(128)S(1)} all-reduce(f32[64]{0:T(128)S(1)} %multiply_reduce_fusion), channel_id=1, replica_groups=mesh['wide'=8,'narrow'=4] {'narrow'}, use_global_device_ids=true, to_apply=%region_12.13 | all-reduce | flops 64 | bytes 512 | tf_op jit(solution)/shard_map/psum | solution.py:35
  566.3 0.1 fusion.38
  566.4 12.1 %all-reduce.1 = f32[512]{0:T(512)S(1)} all-reduce(f32[512]{0:T(512)S(1)} %get-tuple-element.31), channel_id=1, replica_groups=mesh['wide'=8,'narrow'=4] {'wide'}, use_global_device_ids=true, to_apply=%add.1 | all-reduce | flops 512 | bytes 4096
  578.5 2.0 broadcast_divide_fusion
  580.5 12.3 %all-gather.7.cloned.1.call-done = f32[512,2304]{1,0:T(8,128)} async-done(((f32[64,2304]{1,0:T(8,128)}), f32[512,2304]{1,0:T(8,128)}) %all-gather.7.cloned.1.call-update) | async-done | bytes 4718608 | tf_op jit(solution)/shard_map/all_gather | solution.py:39
  592.8 24.1 %fusion = f32[1152,2304]{1,0:T(8,128)} fusion(f32[512,2304]{1,0:T(8,128)} %all-gather.7.cloned.1.call-done, f32[1152,2304]{1,0:T(8,128)} %param.3, bf16[1152,2304]{1,0:T(8,128)(2,1)} %param.4, f32[128,1152]{1,0:T(8,128)S(1)} %fusion.24, f32[128,1152]{1,0:T(8,128)S(1)} %copy-done.1, f32[128,1152]{1,0:T(8,128)S(1)} %fusion.27, f32[128,1152]{1,0:T(8,128)S(1)} %fusion.14), kind=kOutput, calls=%fused_computation.3 | convolution fusion | flops 16319840256 | bytes 33619968 | tf_op jit(solution)/shard_map/dot_general | solution.py:17
  616.9 20.7 %convolution_convert_fusion = bf16[1152,2304]{1,0:T(8,128)(2,1)} fusion(f32[512,2304]{1,0:T(8,128)S(1)} %copy-done.2, f32[512]{0:T(512)S(1)} %all-reduce.1, f32[128,1152]{1,0:T(8,128)S(1)} %fusion.24, f32[128,1152]{1,0:T(8,128)S(1)} %copy-done.1, f32[128,1152]{1,0:T(8,128)S(1)} %fusion.27, f32[128,1152]{1,0:T(8,128)S(1)} %fusion.14), kind=kOutput, calls=%fused_computation.4 | convolution fusion | flops 16313057280 | bytes 12388352 | tf_op jit(solution)/shard_map/dot_general | solution.py:17
  (38 shorter events, 0.4 us)
Async XLA Ops:
  7.2 44.2 %all-gather.5.cloned.1.call-start = ((), (), s32[]{:S(2)}) async-start(), calls=%async_computation.1 | async-start | bytes 5308416 | tf_op jit(solution)/shard_map/all_gather | solution.py:27
  7.9 233.3 %all-gather.9.cloned.1.call-start = ((), (), s32[]{:S(2)}) async-start(), calls=%async_computation.5 | async-start | bytes 11796480 | tf_op jit(solution)/shard_map/all_gather | solution.py:23
  74.3 232.4 %all-reduce.4.cloned.1.call-start = ((), (), s32[]{:S(2)}) async-start(), calls=%async_computation.2 | async-start | bytes 2097152 | tf_op jit(solution)/shard_map/psum | solution.py:29
  251.7 300.5 %reduce-scatter.2.cloned.1.call-start = ((), (), s32[]{:S(2)}) async-start(), calls=%async_computation.3 | async-start | bytes 5308416 | tf_op jit(solution)/shard_map/reduce_scatter | solution.py:32
  306.7 2.6 copy-start.3
  310.8 1.0 copy-start.4
  336.0 0.7 copy-start.5
  462.2 0.8 copy-start.6
  462.2 13.6 %slice-start = ((s8[5308416]{0:T(1024)(128)(4,1)}), s8[4194304]{0:T(1024)(128)(4,1)S(1)}, s32[]{:S(2)}) async-start(s8[5308416]{0:T(1024)(128)(4,1)} %bitcast.59), calls=%async_computation.6 | async-start | bytes 8388608
  465.4 4.7 copy-start.7
  467.0 8.8 %slice-start.1 = ((s8[5308416]{0:T(1024)(128)(4,1)}), s8[1114112]{0:T(1024)(128)(4,1)S(1)}, s32[]{:S(2)}) async-start(s8[5308416]{0:T(1024)(128)(4,1)} %bitcast.59), calls=%async_computation.7 | async-start | bytes 2228224
  470.8 5.0 copy-start
  498.9 53.2 %copy-start.8 = (u32[32]{0:T(128)S(1)}, u32[32]{0:T(128)}, u32[]{:S(2)}) copy-start(u32[32]{0:T(128)} %constant.172) | copy-start | bytes 388
  499.0 93.8 %copy-start.1 = (f32[128,1152]{1,0:T(8,128)S(1)}, f32[128,1152]{1,0:T(8,128)}, u32[]{:S(2)}) copy-start(f32[128,1152]{1,0:T(8,128)} %copy-done) | copy-start | bytes 1769476
  499.0 93.8 %all-gather.7.cloned.1.call-start = ((), (), s32[]{:S(2)}) async-start(), calls=%async_computation.4 | async-start | bytes 5308416 | tf_op jit(solution)/shard_map/all_gather | solution.py:39
  592.8 24.1 %copy-start.2 = (f32[512,2304]{1,0:T(8,128)S(1)}, f32[512,2304]{1,0:T(8,128)}, u32[]{:S(2)}) copy-start(f32[512,2304]{1,0:T(8,128)} %all-gather.7.cloned.1.call-done) | copy-start | bytes 14155780
Sparse Core Ops, SparseCore 0:
  9.9 41.4 all-gather.4
  74.4 166.7 all-gather.8
  251.8 54.8 all-reduce.3
  499.1 53.0 reduce-scatter.1
  553.9 38.8 all-gather.6
